TPU v7x, 32 devices: a whole 2x2x4 slice. The times are simulated.
32 devices in a mesh: shard: 16 (over z, x, core), task: 2 (over y).
Axes of the slice: x: 2, y: 2, z: 4, core: 2. Of those that a mesh axis runs over, the one named last changes fastest.
Arguments:
- task_deltas: bfloat16 [2, 4, 256, 16384], P('task', None, 'shard')
- rank_scores: int32 [2, 4, 256, 16384], P('task', None, 'shard'), may hold values from 0 to 1073741823
- keep_limits: int32 [2, 4, 8], P('task'), may hold values from 268435456 to 805306367
Outputs:
- merged: bfloat16 [4, 256, 16384], P(None, 'shard', 'task')
All inputs are finite; a program needn't handle non-finite values.
Results may differ from a plain program's by a relative error of at most 0.0051.
Values may be sent and summed in bfloat16 or wider, within the bound.
No kernel may reach another device: no remote copies, remote signals or barrier semaphores. Data moves between devices by JAX's collectives and lax.ppermute only.
A program may use at most 64 MiB of HBM per device.

v0:
```python
import jax
import jax.numpy as jnp
from jax import lax
from jax.sharding import PartitionSpec as P

EXPERTS = 8
FF = 16384


def swapped(value, axis, stride):
    mask = 2**stride
    pairs = [(source, source ^ mask) for source in range(lax.axis_size(axis))]
    return lax.ppermute(value, axis, pairs)


def keep_probability(column_sums, grand_sum, row_total):
    column_mean = column_sums / row_total
    grand_mean = grand_sum / (EXPERTS * row_total * FF)
    return (0.2 + 0.7 * column_mean / (column_mean + grand_mean)).astype(jnp.bfloat16)


def on_device(task_deltas, rank_scores, keep_limits):
    groups = lax.axis_size("shard") // EXPERTS
    expert = lax.axis_index("shard") // groups
    row_count = task_deltas.shape[2]
    rows_whole = row_count * groups
    width_all = task_deltas.shape[3]
    selector = jnp.arange(EXPERTS, dtype=jnp.int32) == expert
    results = []
    for layer_at in range(task_deltas.shape[1]):
        change = task_deltas[0, layer_at].astype(jnp.float32)
        magnitude = jnp.sum(jnp.abs(change), axis=0)
        group_total = magnitude
        for bit_at in range(groups.bit_length() - 1):
            group_total = group_total + swapped(group_total, "shard", bit_at)
        grand_sum = lax.psum(jnp.sum(magnitude), "shard")
        rounded = lax.optimization_barrier(keep_probability(group_total, grand_sum, rows_whole))
        probability = rounded.astype(jnp.float32)
        own_limit = jnp.sum(jnp.where(selector, keep_limits[0, layer_at], 0))
        retained = jnp.where(
            rank_scores[0, layer_at] < own_limit, change / probability[None, :], jnp.float32(0.0)
        )
        summed = lax.psum(retained, "task")
        columns = width_all // lax.axis_size("task")
        portion = lax.dynamic_slice_in_dim(summed, lax.axis_index("task") * columns, columns, 1)
        results.append(portion.astype(jnp.bfloat16))
    return jnp.stack(results)


def solution(mesh):
    return jax.shard_map(
        on_device,
        mesh=mesh,
        in_specs=(
            P("task", None, "shard", None),
            P("task", None, "shard", None),
            P("task", None, None),
        ),
        out_specs=P(None, "shard", "task"),
        check_vma=False,
    )
```

profile of v0, /device:TPU:0, one launch (start us, length us, event | category | flops | bytes accessed | tf_op | source)
XLA Modules:
  0.0 146.4 jit_solution(15803664491565942427)
XLA Ops:
  0.0 0.0 copy-start
  0.0 0.0 copy-start.1
  0.0 3.3 %fusion = (f32[]{:T(128)}, f32[]{:T(128)}, f32[]{:T(128)}, f32[]{:T(128)}, f32[16384]{0:T(1024)S(1)}, /*index=5*/f32[16384]{0:T(1024)S(1)}, f32[16384]{0:T(1024)S(1)}, f32[16384]{0:T(1024)S(1)}) fusion(bf16[1,4,16,16384]{3,2,1,0:T(8,128)(2,1)} %param.3), kind=kLoop, calls=%fused_computation.8 | loop fusion | flops 4128764 | bytes 2359312 | tf_op jit(solution)/shard_map/reduce_sum | solution.py:36
  3.3 0.5 collective-permute-start.1
  3.8 0.0 collective-permute-start
  3.8 0.5 collective-permute-start.3
  4.3 0.0 collective-permute-start.2
  4.3 35.8 %all-reduce = (f32[]{:T(128)}, f32[]{:T(128)}, f32[]{:T(128)}, f32[]{:T(128)}) all-reduce(f32[]{:T(128)} %get-tuple-element.8, f32[]{:T(128)} %get-tuple-element.7, f32[]{:T(128)} %get-tuple-element.6, f32[]{:T(128)} %get-tuple-element.5), channel_id=1, replica_groups=mesh['shard'=16,'task'=2] {'shard'}, use_global_device_ids=true, to_apply=%region_18.19 | all-reduce | flops 4 | bytes 32 | tf_op jit(solution)/shard_map/psum | solution.py:36
  42.6 0.0 copy-done.1
  42.6 0.7 fusion.23
  43.3 0.0 collective-permute-done.1
  43.4 0.0 collective-permute-done
  43.4 0.0 collective-permute-done.3
  43.5 0.0 collective-permute-done.2
  43.5 0.0 copy-done
  43.6 6.6 %fusion.8 = (f32[16,16384]{1,0:T(8,128)S(1)}, f32[16,16384]{1,0:T(8,128)}, f32[16,16384]{1,0:T(8,128)}, f32[16,16384]{1,0:T(8,128)}) fusion(s32[1,4,16,16384]{3,2,1,0:T(8,128)} %param.4, f32[16384]{0:T(1024)S(1)} %convert_element_type.63, s32[]{:T(128)} %get-tuple-element.13, bf16[1,4,16,16384]{3,2,1,0:T(8,128)(2,1)S(1)} %copy-done, ...), kind=kLoop, calls=%fused_computation.16 | loop fusion | flops 4194304 | bytes 10747920 | tf_op jit(solution)/shard_map/jit(_where)/select_n | solution.py:40
  50.2 95.0 %all-reduce.3 = (bf16[16,16384]{1,0:T(8,128)(2,1)S(1)}, bf16[16,16384]{1,0:T(8,128)(2,1)S(1)}, bf16[16,16384]{1,0:T(8,128)(2,1)S(1)}, bf16[16,16384]{1,0:T(8,128)(2,1)S(1)}) all-reduce(f32[16,16384]{1,0:T(8,128)} %get-tuple-element.27, f32[16,16384]{1,0:T(8,128)} %get-tuple-element.28, ...), channel_id=1, replica_groups=mesh['shard'=16,'task'=2] {'task'}, use_global_device_ids=true, to_apply=%region_19.20 | all-reduce | flops 1048576 | bytes 6291456 | tf_op jit(solution)/shard_map/psum | solution.py:43
  145.3 1.1 pad_maximum_fusion
  (10 shorter events, 0.2 us)
Async XLA Ops:
  0.0 43.6 %copy-start = (bf16[1,4,16,16384]{3,2,1,0:T(8,128)(2,1)S(1)}, bf16[1,4,16,16384]{3,2,1,0:T(8,128)(2,1)}, u32[]{:S(2)}) copy-start(bf16[1,4,16,16384]{3,2,1,0:T(8,128)(2,1)} %param.3) | copy-start | bytes 6291460
  0.0 42.6 %copy-start.1 = (s32[1,4,8]{2,1,0:T(4,128)S(1)}, s32[1,4,8]{2,1,0:T(4,128)}, u32[]{:S(2)}) copy-start(s32[1,4,8]{2,1,0:T(4,128)} %param.5) | copy-start | bytes 388
  3.3 40.0 %collective-permute-start.1 = (f32[16384]{0:T(1024)S(1)}, f32[16384]{0:T(1024)S(1)}, u32[]{:S(2)}, u32[]{:S(2)}) collective-permute-start(f32[16384]{0:T(1024)S(1)} %get-tuple-element.9), channel_id=1, source_target_pairs={{0,2},{2,0},{4,6},{6,4},{8,10},{10,8},{12,14},{14,12},{16,18},{18,... | collective-permute-start | bytes 196616 | tf_op jit(solution)/shard_map/ppermute | solution.py:13
  3.8 39.5 %collective-permute-start = (f32[16384]{0:T(1024)S(1)}, f32[16384]{0:T(1024)S(1)}, u32[]{:S(2)}, u32[]{:S(2)}) collective-permute-start(f32[16384]{0:T(1024)S(1)} %get-tuple-element.10), channel_id=1, source_target_pairs={{0,2},{2,0},{4,6},{6,4},{8,10},{10,8},{12,14},{14,12},{16,18},{18,... | collective-permute-start | bytes 196616 | tf_op jit(solution)/shard_map/ppermute | solution.py:13
  3.8 39.6 %collective-permute-start.3 = (f32[16384]{0:T(1024)S(1)}, f32[16384]{0:T(1024)S(1)}, u32[]{:S(2)}, u32[]{:S(2)}) collective-permute-start(f32[16384]{0:T(1024)S(1)} %get-tuple-element.11), channel_id=1, source_target_pairs={{0,2},{2,0},{4,6},{6,4},{8,10},{10,8},{12,14},{14,12},{16,18},{18,... | collective-permute-start | bytes 196616 | tf_op jit(solution)/shard_map/ppermute | solution.py:13
  4.3 39.2 %collective-permute-start.2 = (f32[16384]{0:T(1024)S(1)}, f32[16384]{0:T(1024)S(1)}, u32[]{:S(2)}, u32[]{:S(2)}) collective-permute-start(f32[16384]{0:T(1024)S(1)} %get-tuple-element.12), channel_id=1, source_target_pairs={{0,2},{2,0},{4,6},{6,4},{8,10},{10,8},{12,14},{14,12},{16,18},{18,... | collective-permute-start | bytes 196616 | tf_op jit(solution)/shard_map/ppermute | solution.py:13
where the time goes:
time: 147 us; the launch traced here: 146 us
  blocking collectives  131 us (89%)
  other arithmetic  11.8 us (8%)
  between operations  2.65 us (2%)
    psum x1, blocking collectives, on_device(): summed = lax.psum(retained, 'task')  95 us
    psum x1, blocking collectives, on_device(): grand_sum = lax.psum(jnp.sum(magnitude), 'shard')  35.8 us
    select_n x1, other arithmetic, on_device(): jnp.where(rank_scores[0, layer_at] < own_limit, change / probability[None...  6.62 us
    reduce_sum x1, other arithmetic, on_device(): grand_sum = lax.psum(jnp.sum(magnitude), 'shard')  3.31 us
  transfers between devices with their start and end apart: 4, of which 0 were waited for; matrix products, arithmetic and copies ran while one was open for 1% of the time, Pallas kernels for 0%

commit v1 on v0

--- a/solution.py
+++ b/solution.py
@@ -40,7 +40,8 @@
         retained = jnp.where(
             rank_scores[0, layer_at] < own_limit, change / probability[None, :], jnp.float32(0.0)
         )
-        summed = lax.psum(retained, "task")
+        shards = lax.all_gather(retained, "task", axis=0, tiled=False)
+        summed = shards.sum(axis=0)
         columns = width_all // lax.axis_size("task")
         portion = lax.dynamic_slice_in_dim(summed, lax.axis_index("task") * columns, columns, 1)
         results.append(portion.astype(jnp.bfloat16))

time: 147 us -> 201 us (1.37)
  waiting for transfers between devices: 0.01 us -> 129 us
  blocking collectives: 131 us -> 35.8 us
  between operations: 2.65 us -> 15.8 us
  other arithmetic: 11.8 us -> 19.4 us
    all_gather x0 -> x4, waiting for transfers between devices: none -> 127 us  [on_device(): shards = lax.all_gather(retained, 'task', axis=0, tiled=False)]
    psum x1 -> x0, blocking collectives: 95 us -> none  [on_device(): summed = lax.psum(retained, 'task')]
    reduce_sum x0 -> x4, other arithmetic: none -> 7 us  [on_device(): summed = shards.sum(axis=0)]
  transfers between devices with their start and end apart: 4 -> 8, of which waited for: 0 -> 4; matrix products, arithmetic and copies ran while one was open for 1% -> 3% of each run, Pallas kernels for 0% -> 0%
where the time goes in v1:
time: 201 us
  waiting for transfers between devices  129 us (64%)
  blocking collectives  35.8 us (18%)
  other arithmetic  19.4 us (10%)
  between operations  15.8 us (8%)
    all_gather x4, waiting for transfers between devices, on_device(): shards = lax.all_gather(retained, 'task', axis=0, tiled=False)  127 us
    psum x1, blocking collectives, on_device(): grand_sum = lax.psum(jnp.sum(magnitude), 'shard')  35.8 us
    select_n x1, other arithmetic, on_device(): jnp.where(rank_scores[0, layer_at] < own_limit, change / probability[None...  7.13 us
    reduce_sum x4, other arithmetic, on_device(): summed = shards.sum(axis=0)  7 us
  transfers between devices with their start and end apart: 8, of which 4 were waited for; matrix products, arithmetic and copies ran while one was open for 3% of the time, Pallas kernels for 0%

profile of v1, /device:TPU:0, one launch (start us, length us, event | category | flops | bytes accessed | tf_op | source)
XLA Modules:
  0.0 201.1 jit_solution(18045789110461857311)
XLA Ops:
  6.5 0.0 copy-start
  6.5 0.0 copy-start.1
  6.5 0.0 all-gather.5.cloned.1.call-start
  6.5 3.3 %fusion = (f32[]{:T(128)}, f32[16384]{0:T(1024)S(1)}, f32[16384]{0:T(1024)S(1)}, f32[]{:T(128)}, f32[16384]{0:T(1024)S(1)}, /*index=5*/f32[]{:T(128)}, f32[16384]{0:T(1024)S(1)}, f32[]{:T(128)}) fusion(bf16[1,4,16,16384]{3,2,1,0:T(8,128)(2,1)} %param.3), kind=kLoop, calls=%fused_computation.8 | loop fusion | flops 4128764 | bytes 2359312 | tf_op jit(solution)/shard_map/reduce_sum | solution.py:36
  9.9 0.5 collective-permute-start
  10.3 0.0 collective-permute-start.1
  10.4 0.5 collective-permute-start.2
  10.9 0.0 collective-permute-start.3
  10.9 35.8 %all-reduce = (f32[]{:T(128)}, f32[]{:T(128)}, f32[]{:T(128)}, f32[]{:T(128)}) all-reduce(f32[]{:T(128)} %get-tuple-element.12, f32[]{:T(128)} %get-tuple-element.10, f32[]{:T(128)} %get-tuple-element.8, f32[]{:T(128)} %get-tuple-element.5), channel_id=1, replica_groups=mesh['shard'=16,'task'=2] {'shard'}, use_global_device_ids=true, to_apply=%region_18.19 | all-reduce | flops 4 | bytes 32 | tf_op jit(solution)/shard_map/psum | solution.py:36
  49.2 0.0 copy-done.1
  49.2 0.7 fusion.27
  49.9 0.0 collective-permute-done
  50.0 0.0 collective-permute-done.1
  50.0 0.0 collective-permute-done.2
  50.1 0.0 collective-permute-done.3
  50.1 0.0 copy-done
  50.2 7.1 %fusion.9 = (f32[1,16,16384]{2,1,0:T(8,128)}, f32[1,16,16384]{2,1,0:T(8,128)}, f32[1,16,16384]{2,1,0:T(8,128)}, f32[1,16,16384]{2,1,0:T(8,128)}) fusion(s32[1,4,16,16384]{3,2,1,0:T(8,128)} %param.4, f32[16384]{0:T(1024)S(1)} %convert_element_type.104, s32[]{:T(128)} %get-tuple-element.13, bf16[1,4,16,16384]{3,2,1,0:T(8,128)(2,1)S(1)} %copy-done, ...), kind=kLoop, calls=%fused_computation.17 | loop fusion | flops 4194304 | bytes 10747920 | tf_op jit(solution)/shard_map/jit(_where)/select_n | solution.py:40
  57.3 0.0 all-gather.5.cloned.1.call-update
  57.3 0.0 all-gather.7.cloned.1.call-start
  57.4 0.7 all-gather.7.cloned.1.call-update
  58.1 0.0 all-gather.11.cloned.1.call-start
  58.1 0.7 all-gather.11.cloned.1.call-update
  58.8 0.0 all-gather.9.cloned.1.call-start
  58.9 0.5 all-gather.9.cloned.1.call-update
  59.4 28.5 %all-gather.5.cloned.1.call-done = f32[2,16,16384]{2,1,0:T(8,128)} async-done(((f32[1,16,16384]{2,1,0:T(8,128)}), f32[2,16,16384]{2,1,0:T(8,128)}) %all-gather.5.cloned.1.call-update) | async-done | bytes 2097168 | tf_op jit(solution)/shard_map/all_gather | solution.py:43
  87.8 1.7 reduce_sum.147
  89.6 32.9 %all-gather.7.cloned.1.call-done = f32[2,16,16384]{2,1,0:T(8,128)} async-done(((f32[1,16,16384]{2,1,0:T(8,128)}), f32[2,16,16384]{2,1,0:T(8,128)}) %all-gather.7.cloned.1.call-update) | async-done | bytes 2097168 | tf_op jit(solution)/shard_map/all_gather | solution.py:43
  122.5 1.7 reduce_sum.151
  124.3 32.9 %all-gather.11.cloned.1.call-done = f32[2,16,16384]{2,1,0:T(8,128)} async-done(((f32[1,16,16384]{2,1,0:T(8,128)}), f32[2,16,16384]{2,1,0:T(8,128)}) %all-gather.11.cloned.1.call-update) | async-done | bytes 2097168 | tf_op jit(solution)/shard_map/all_gather | solution.py:43
  157.2 1.7 reduce_sum.159
  159.0 32.7 %all-gather.9.cloned.1.call-done = f32[2,16,16384]{2,1,0:T(8,128)} async-done(((f32[1,16,16384]{2,1,0:T(8,128)}), f32[2,16,16384]{2,1,0:T(8,128)}) %all-gather.9.cloned.1.call-update) | async-done | bytes 2097168 | tf_op jit(solution)/shard_map/all_gather | solution.py:43
  191.7 1.7 reduce_sum.155
  193.5 1.1 pad_maximum_fusion
  (12 shorter events, 0.2 us)
Async XLA Ops:
  6.5 43.6 %copy-start = (bf16[1,4,16,16384]{3,2,1,0:T(8,128)(2,1)S(1)}, bf16[1,4,16,16384]{3,2,1,0:T(8,128)(2,1)}, u32[]{:S(2)}) copy-start(bf16[1,4,16,16384]{3,2,1,0:T(8,128)(2,1)} %param.3) | copy-start | bytes 6291460
  6.5 42.6 %copy-start.1 = (s32[1,4,8]{2,1,0:T(4,128)S(1)}, s32[1,4,8]{2,1,0:T(4,128)}, u32[]{:S(2)}) copy-start(s32[1,4,8]{2,1,0:T(4,128)} %param.5) | copy-start | bytes 388
  6.5 81.3 %all-gather.5.cloned.1.call-start = ((), (), s32[]{:S(2)}) async-start(), calls=%async_computation | async-start | bytes 3145728 | tf_op jit(solution)/shard_map/all_gather | solution.py:43
  9.9 40.1 %collective-permute-start = (f32[16384]{0:T(1024)S(1)}, f32[16384]{0:T(1024)S(1)}, u32[]{:S(2)}, u32[]{:S(2)}) collective-permute-start(f32[16384]{0:T(1024)S(1)} %get-tuple-element.6), channel_id=1, source_target_pairs={{0,2},{2,0},{4,6},{6,4},{8,10},{10,8},{12,14},{14,12},{16,18},{18,... | collective-permute-start | bytes 196616 | tf_op jit(solution)/shard_map/ppermute | solution.py:13
  10.3 39.6 %collective-permute-start.1 = (f32[16384]{0:T(1024)S(1)}, f32[16384]{0:T(1024)S(1)}, u32[]{:S(2)}, u32[]{:S(2)}) collective-permute-start(f32[16384]{0:T(1024)S(1)} %get-tuple-element.7), channel_id=1, source_target_pairs={{0,2},{2,0},{4,6},{6,4},{8,10},{10,8},{12,14},{14,12},{16,18},{18,... | collective-permute-start | bytes 196616 | tf_op jit(solution)/shard_map/ppermute | solution.py:13
  10.4 39.6 %collective-permute-start.2 = (f32[16384]{0:T(1024)S(1)}, f32[16384]{0:T(1024)S(1)}, u32[]{:S(2)}, u32[]{:S(2)}) collective-permute-start(f32[16384]{0:T(1024)S(1)} %get-tuple-element.9), channel_id=1, source_target_pairs={{0,2},{2,0},{4,6},{6,4},{8,10},{10,8},{12,14},{14,12},{16,18},{18,... | collective-permute-start | bytes 196616 | tf_op jit(solution)/shard_map/ppermute | solution.py:13
  10.9 39.2 %collective-permute-start.3 = (f32[16384]{0:T(1024)S(1)}, f32[16384]{0:T(1024)S(1)}, u32[]{:S(2)}, u32[]{:S(2)}) collective-permute-start(f32[16384]{0:T(1024)S(1)} %get-tuple-element.11), channel_id=1, source_target_pairs={{0,2},{2,0},{4,6},{6,4},{8,10},{10,8},{12,14},{14,12},{16,18},{18,... | collective-permute-start | bytes 196616 | tf_op jit(solution)/shard_map/ppermute | solution.py:13
  57.3 65.2 %all-gather.7.cloned.1.call-start = ((), (), s32[]{:S(2)}) async-start(), calls=%async_computation.1 | async-start | bytes 3145728 | tf_op jit(solution)/shard_map/all_gather | solution.py:43
  58.1 99.1 %all-gather.11.cloned.1.call-start = ((), (), s32[]{:S(2)}) async-start(), calls=%async_computation.3 | async-start | bytes 3145728 | tf_op jit(solution)/shard_map/all_gather | solution.py:43
  58.8 132.9 %all-gather.9.cloned.1.call-start = ((), (), s32[]{:S(2)}) async-start(), calls=%async_computation.2 | async-start | bytes 3145728 | tf_op jit(solution)/shard_map/all_gather | solution.py:43
Sparse Core Ops, SparseCore 0:
  57.4 30.3 all-gather.4
  89.4 33.0 all-gather.6
  124.1 33.0 all-gather.10
  158.6 33.0 all-gather.8
